TPU v7x, 256 devices: a whole 4x4x8 slice. The times are simulated.
256 devices in a mesh: expert: 8 (over x, core), shard: 32 (over z, y).
Axes of the slice: x: 4, y: 4, z: 8, core: 2. Of those that a mesh axis runs over, the one named last changes fastest.
Arguments:
- train_down: float32 [16, 6400, 4096], P('expert', None, 'shard'), may hold values from -0.15625 to 0.15625
- other_down: bfloat16 [16, 6400, 4096], P('expert', None, 'shard'), may hold values from -0.0390625 to 0.0390625
- router_weight: float32 [4096, 16], P('shard', 'expert'), may hold values from -0.09375 to 0.09375
- router_gain: float32 [4096], P('shard'), may hold values from 0.25 to 1.75
Outputs:
- ready_down: bfloat16 [16, 6400, 4096], P('expert', 'shard')
- scale_down: float32 [16, 6400], P('expert', 'shard')
- serve_router: bfloat16 [4096, 16], replicated
All inputs are finite; a program needn't handle non-finite values. Where the computation divides by a largest or mean magnitude, that divisor is 1e-20 or more.
Results may differ from a plain program's by a relative error of at most 0.001.
Values may be sent and summed in bfloat16 or wider, within the bound.
A program may use at most 64 MiB of HBM per device.

v0:
```python
import jax
import jax.numpy as jnp
from jax import lax
from jax.sharding import PartitionSpec as P


def sent_to_all(x, axis):
    copies = jnp.broadcast_to(x, (lax.axis_size(axis), *x.shape))
    return lax.all_to_all(copies, axis, split_axis=0, concat_axis=0, tiled=True)


def of_everyone(x, axis):
    everything = sent_to_all(x, axis)
    return jnp.max(everything, axis=0)


def laid_out(parts, dim):
    lengths = list(parts.shape[1:])
    lengths[dim] *= parts.shape[0]
    return jnp.moveaxis(parts, 0, dim).reshape(lengths)


def gathered_copies(x, axis, dim):
    return laid_out(sent_to_all(x, axis), dim)


def per_device(train_down, other_down, router_weight, router_gain):
    latest_down = train_down + other_down.astype(jnp.float32)
    scale_down = of_everyone(jnp.max(jnp.abs(latest_down), axis=2), "shard")
    narrow_down = (latest_down / jnp.expand_dims(scale_down, 2)).astype(jnp.bfloat16)
    ready_down = lax.all_to_all(narrow_down, "shard", split_axis=1, concat_axis=2, tiled=True)
    scale_down = lax.dynamic_slice_in_dim(
        scale_down, lax.axis_index("shard") * ready_down.shape[1], ready_down.shape[1], axis=1
    )
    part_router = (router_weight * router_gain[:, None]).astype(jnp.bfloat16)
    row_router = gathered_copies(part_router, "shard", 0)
    serve_router = gathered_copies(row_router, "expert", 1)
    return (ready_down, scale_down, serve_router)


def solution(mesh):
    in_specs = (
        P("expert", None, "shard"),
        P("expert", None, "shard"),
        P("shard", "expert"),
        P("shard"),
    )
    out_specs = (P("expert", "shard", None), P("expert", "shard"), P())
    return jax.shard_map(
        per_device, mesh=mesh, in_specs=in_specs, out_specs=out_specs, check_vma=False
    )
```

profile of v0, /device:TPU:9, one launch (start us, length us, event | category | flops | bytes accessed | tf_op | source)
XLA Modules:
  0.0 201.1 jit_solution(1283728771421727400)
XLA Ops:
  0.6 0.7 multiply_convert_fusion
  1.3 0.6 broadcast_in_dim.12
  1.9 11.1 %all-to-all-start.2 = ((bf16[32,128,2]{1,2,0:T(2,128)(2,1)}), bf16[32,128,2]{1,2,0:T(2,128)(2,1)S(1)}, u32[]{:S(2)}, u32[]{:S(2)}) async-start(bf16[32,128,2]{1,2,0:T(2,128)(2,1)} %broadcast_in_dim.12), calls=%async_computation.2 | async-start | bytes 32768 | tf_op jit(solution)/shard_map/all_to_all | solution.py:9
  13.1 5.6 %abs_reduce_fusion = f32[2,6400]{1,0:T(2,128)S(1)} fusion(f32[2,6400,128]{2,1,0:T(8,128)} %param.4, bf16[2,6400,128]{2,1,0:T(8,128)(2,1)} %param.5), kind=kLoop, calls=%fused_computation.1 | loop fusion | flops 6540800 | bytes 9881600 | tf_op jit(solution)/shard_map/reduce_max | solution.py:29
  18.7 0.0 copy-start
  18.7 2.0 all-to-all-done.2
  20.7 0.4 broadcast_in_dim.11
  21.1 46.8 %all_to_all.33 = f32[32,2,6400]{2,1,0:T(2,128)} all-to-all(f32[32,2,6400]{2,1,0:T(2,128)S(1)} %broadcast_in_dim.11), channel_id=1, replica_groups=mesh['expert'=8,'shard'=32] {'shard'}, dimensions={0} | all-to-all | bytes 3276800 | tf_op jit(solution)/shard_map/all_to_all | solution.py:9
  67.9 0.7 broadcast_in_dim.13
  68.6 6.7 %all-to-all-start.3 = ((bf16[8,4096,2]{1,2,0:T(2,128)(2,1)}), bf16[8,4096,2]{1,2,0:T(2,128)(2,1)S(1)}, u32[]{:S(2)}, u32[]{:S(2)}) async-start(bf16[8,4096,2]{1,2,0:T(2,128)(2,1)} %broadcast_in_dim.13), calls=%async_computation.3 | async-start | bytes 262144 | tf_op jit(solution)/shard_map/all_to_all | solution.py:9
  75.4 1.9 reduce_max.19
  77.3 0.0 copy-done
  77.3 4.7 %divide_convert_fusion = bf16[2,6400,128]{2,1,0:T(8,128)(2,1)S(1)} fusion(f32[2,6400,128]{2,1,0:T(8,128)} %param.4, bf16[2,6400,128]{2,1,0:T(8,128)(2,1)S(1)} %copy-done, f32[2,6400]{1,0:T(2,128)S(1)} %reduce_max.19), kind=kLoop, calls=%fused_computation | loop fusion | flops 6553600 | bytes 13158400 | tf_op jit(solution)/shard_map/convert_element_type | solution.py:30
  82.0 27.9 %copy.31 = bf16[2,6400,128]{2,0,1:T(2,128)(2,1)} copy(bf16[2,6400,128]{2,1,0:T(8,128)(2,1)S(1)} %divide_convert_fusion) | data formatting | bytes 6553600 | tf_op jit(solution)/shard_map/convert_element_type | solution.py:30
  109.9 0.0 all-to-all-done.3
  109.9 5.0 %all-to-all-start.1 = ((bf16[2,6400,128]{2,0,1:T(2,128)(2,1)}), bf16[2,6400,128]{2,0,1:T(2,128)(2,1)S(1)}, u32[]{:S(2)}, u32[]{:S(2)}) async-start(bf16[2,6400,128]{2,0,1:T(2,128)(2,1)} %copy.31), calls=%async_computation.1 | async-start | bytes 6553600 | tf_op jit(solution)/shard_map/all_to_all | solution.py:31
  114.9 0.7 reshape.15
  115.6 0.7 constant_dynamic-slice_fusion
  116.3 76.1 %all-to-all-done.1 = bf16[2,6400,128]{2,0,1:T(2,128)(2,1)S(1)} async-done(((bf16[2,6400,128]{2,0,1:T(2,128)(2,1)}), bf16[2,6400,128]{2,0,1:T(2,128)(2,1)S(1)}, u32[]{:S(2)}, u32[]{:S(2)}) %all-to-all-start.1) | async-done | bytes 3276832 | tf_op jit(solution)/shard_map/all_to_all | solution.py:31
  192.4 2.5 %copy.32 = bf16[2,200,32,128]{3,2,1,0:T(8,128)(2,1)} copy(bf16[2,200,32,128]{3,0,1,2:T(2,128)(2,1)S(1)} %bitcast.9) | data formatting | bytes 6553600 | tf_op jit(solution)/shard_map/all_to_all | solution.py:31
  194.9 6.2 %all_to_all.26 = bf16[2,200,4096]{2,1,0:T(8,128)(2,1)} reshape(bf16[2,200,32,128]{3,2,1,0:T(8,128)(2,1)} %copy.32) | data formatting | bytes 6553600 | tf_op jit(solution)/shard_map/all_to_all | solution.py:31
Async XLA Ops:
  1.9 18.8 %all-to-all-start.2 = ((bf16[32,128,2]{1,2,0:T(2,128)(2,1)}), bf16[32,128,2]{1,2,0:T(2,128)(2,1)S(1)}, u32[]{:S(2)}, u32[]{:S(2)}) async-start(bf16[32,128,2]{1,2,0:T(2,128)(2,1)} %broadcast_in_dim.12), calls=%async_computation.2 | async-start | bytes 32768 | tf_op jit(solution)/shard_map/all_to_all | solution.py:9
  18.7 58.6 %copy-start = (bf16[2,6400,128]{2,1,0:T(8,128)(2,1)S(1)}, bf16[2,6400,128]{2,1,0:T(8,128)(2,1)}, u32[]{:S(2)}) copy-start(bf16[2,6400,128]{2,1,0:T(8,128)(2,1)} %param.5) | copy-start | bytes 9830404
  68.6 41.3 %all-to-all-start.3 = ((bf16[8,4096,2]{1,2,0:T(2,128)(2,1)}), bf16[8,4096,2]{1,2,0:T(2,128)(2,1)S(1)}, u32[]{:S(2)}, u32[]{:S(2)}) async-start(bf16[8,4096,2]{1,2,0:T(2,128)(2,1)} %broadcast_in_dim.13), calls=%async_computation.3 | async-start | bytes 262144 | tf_op jit(solution)/shard_map/all_to_all | solution.py:9
  109.9 82.5 %all-to-all-start.1 = ((bf16[2,6400,128]{2,0,1:T(2,128)(2,1)}), bf16[2,6400,128]{2,0,1:T(2,128)(2,1)S(1)}, u32[]{:S(2)}, u32[]{:S(2)}) async-start(bf16[2,6400,128]{2,0,1:T(2,128)(2,1)} %copy.31), calls=%async_computation.1 | async-start | bytes 6553600 | tf_op jit(solution)/shard_map/all_to_all | solution.py:31
where the time goes:
time: 202 us; the launch traced here: 201 us
  waiting for transfers between devices  78.1 us (39%)
  blocking collectives  46.8 us (23%)
  local copies, waits for them, and re-layouts  39.7 us (20%)
  starting transfers between devices  22.9 us (11%)
  other arithmetic  12.9 us (6%)
    all_to_all x1, waiting for transfers between devices, per_device(): lax.all_to_all(narrow_down, 'shard', split_axis=1, concat_axis=2, tiled=T...  76.1 us
    all_to_all x1, blocking collectives, sent_to_all(): return lax.all_to_all(copies, axis, split_axis=0, concat_axis=0, tiled=True)  46.8 us
    convert_element_type x1, local copies, waits for them, and re-layouts, per_device(): (latest_down / jnp.expand_dims(scale_down, 2)).astype(jnp.bfloat16)  27.9 us
    all_to_all x2, starting transfers between devices, sent_to_all(): return lax.all_to_all(copies, axis, split_axis=0, concat_axis=0, tiled=True)  17.8 us
    all_to_all x2, local copies, waits for them, and re-layouts, per_device(): lax.all_to_all(narrow_down, 'shard', split_axis=1, concat_axis=2, tiled=T...  8.72 us
    reduce_max x1, other arithmetic, per_device(): scale_down = of_everyone(jnp.max(jnp.abs(latest_down), axis=2), 'shard')  5.6 us
    all_to_all x1, starting transfers between devices, per_device(): lax.all_to_all(narrow_down, 'shard', split_axis=1, concat_axis=2, tiled=T...  5.01 us
    convert_element_type x1, other arithmetic, per_device(): (latest_down / jnp.expand_dims(scale_down, 2)).astype(jnp.bfloat16)  4.74 us
  transfers between devices with their start and end apart: 3, of which 2 were waited for; matrix products, arithmetic and copies ran while one was open for 21% of the time, Pallas kernels for 0%

commit v1 on v0

--- a/solution.py
+++ b/solution.py
@@ -28,7 +28,12 @@
     latest_down = train_down + other_down.astype(jnp.float32)
     scale_down = of_everyone(jnp.max(jnp.abs(latest_down), axis=2), "shard")
     narrow_down = (latest_down / jnp.expand_dims(scale_down, 2)).astype(jnp.bfloat16)
-    ready_down = lax.all_to_all(narrow_down, "shard", split_axis=1, concat_axis=2, tiled=True)
+    ready_down = jnp.concatenate(
+        lax.all_to_all(
+            jnp.stack(jnp.split(narrow_down, lax.axis_size("shard"), axis=1)), "shard", 0, 0
+        ),
+        axis=2,
+    )
     scale_down = lax.dynamic_slice_in_dim(
         scale_down, lax.axis_index("shard") * ready_down.shape[1], ready_down.shape[1], axis=1
     )

time: 202 us -> 169 us (0.84)
  local copies, waits for them, and re-layouts: 39.7 us -> 7.53 us
    convert_element_type x1 -> x0, local copies, waits for them, and re-layouts: 27.9 us -> none  [per_device(): (latest_down / jnp.expand_dims(scale_down, 2)).astype(jnp.bfloat16)]
    all_to_all x2 -> x0, local copies, waits for them, and re-layouts: 8.72 us -> none  [per_device(): lax.all_to_all(narrow_down, 'shard', split_axis=1, concat_axis=2, tiled=T...]
    unnamed x2 -> x35, local copies, waits for them, and re-layouts: 0.01 us -> 2.25 us
    reshape x0 -> x1, local copies, waits for them, and re-layouts: none -> 2.14 us  [per_device(): jnp.concatenate(lax.all_to_all(jnp.stack(jnp.split(narrow_down, lax.axis_...]
  transfers between devices with their start and end apart: 3 -> 3, of which waited for: 2 -> 2; matrix products, arithmetic and copies ran while one was open for 21% -> 8% of each run, Pallas kernels for 0% -> 0%
where the time goes in v1:
time: 169 us
  waiting for transfers between devices  78.1 us (46%)
  blocking collectives  46.8 us (28%)
  starting transfers between devices  22.9 us (14%)
  other arithmetic  12.9 us (8%)
  local copies, waits for them, and re-layouts  7.53 us (4%)
    all_to_all x1, waiting for transfers between devices, per_device(): lax.all_to_all(jnp.stack(jnp.split(narrow_down, lax.axis_size('shard'), a...  76.1 us
    all_to_all x1, blocking collectives, sent_to_all(): return lax.all_to_all(copies, axis, split_axis=0, concat_axis=0, tiled=True)  46.8 us
    all_to_all x2, starting transfers between devices, sent_to_all(): return lax.all_to_all(copies, axis, split_axis=0, concat_axis=0, tiled=True)  17.8 us
    reduce_max x1, other arithmetic, per_device(): scale_down = of_everyone(jnp.max(jnp.abs(latest_down), axis=2), 'shard')  5.6 us
    all_to_all x1, starting transfers between devices, per_device(): lax.all_to_all(jnp.stack(jnp.split(narrow_down, lax.axis_size('shard'), a...  5.01 us
    convert_element_type x1, other arithmetic, per_device(): (latest_down / jnp.expand_dims(scale_down, 2)).astype(jnp.bfloat16)  4.74 us
  transfers between devices with their start and end apart: 3, of which 2 were waited for; matrix products, arithmetic and copies ran while one was open for 8% of the time, Pallas kernels for 0%

profile of v1, /device:TPU:9, one launch (start us, length us, event | category | flops | bytes accessed | tf_op | source)
XLA Modules:
  0.0 169.1 jit_solution(7231324775538372856)
XLA Ops:
  0.6 0.7 multiply_convert_fusion
  1.3 0.6 broadcast_in_dim.12
  1.9 11.1 %all-to-all-start.2 = ((bf16[32,128,2]{1,2,0:T(2,128)(2,1)}), bf16[32,128,2]{1,2,0:T(2,128)(2,1)S(1)}, u32[]{:S(2)}, u32[]{:S(2)}) async-start(bf16[32,128,2]{1,2,0:T(2,128)(2,1)} %broadcast_in_dim.12), calls=%async_computation.2 | async-start | bytes 32768 | tf_op jit(solution)/shard_map/all_to_all | solution.py:9
  13.1 5.6 %abs_reduce_fusion = f32[2,6400]{1,0:T(2,128)S(1)} fusion(f32[2,6400,128]{2,1,0:T(8,128)} %param.4, bf16[2,6400,128]{2,1,0:T(8,128)(2,1)} %param.5), kind=kLoop, calls=%fused_computation.1 | loop fusion | flops 6540800 | bytes 9881600 | tf_op jit(solution)/shard_map/reduce_max | solution.py:29
  18.7 0.0 copy-start
  18.7 2.0 %all-to-all-done.2 = bf16[32,128,2]{1,2,0:T(2,128)(2,1)S(1)} async-done(((bf16[32,128,2]{1,2,0:T(2,128)(2,1)}), bf16[32,128,2]{1,2,0:T(2,128)(2,1)S(1)}, u32[]{:S(2)}, u32[]{:S(2)}) %all-to-all-start.2) | async-done | bytes 16416 | tf_op jit(solution)/shard_map/all_to_all | solution.py:9
  20.7 0.4 broadcast_in_dim.11
  21.1 46.8 %all_to_all.20 = f32[32,2,6400]{2,1,0:T(2,128)} all-to-all(f32[32,2,6400]{2,1,0:T(2,128)S(1)} %broadcast_in_dim.11), channel_id=1, replica_groups=mesh['expert'=8,'shard'=32] {'shard'}, dimensions={0} | all-to-all | bytes 3276800 | tf_op jit(solution)/shard_map/all_to_all | solution.py:9
  67.9 0.7 broadcast_in_dim.13
  68.6 6.7 %all-to-all-start.3 = ((bf16[8,4096,2]{1,2,0:T(2,128)(2,1)}), bf16[8,4096,2]{1,2,0:T(2,128)(2,1)S(1)}, u32[]{:S(2)}, u32[]{:S(2)}) async-start(bf16[8,4096,2]{1,2,0:T(2,128)(2,1)} %broadcast_in_dim.13), calls=%async_computation.3 | async-start | bytes 262144 | tf_op jit(solution)/shard_map/all_to_all | solution.py:9
  75.4 1.9 %reduce_max.19 = f32[2,6400]{1,0:T(2,128)S(1)} reduce(f32[32,2,6400]{2,1,0:T(2,128)} %all_to_all.20, f32[]{:T(128)} %constant.5.clone.1), dimensions={0}, to_apply=%region_1.0 | reduce | flops 396800 | bytes 1689604 | tf_op jit(solution)/shard_map/reduce_max | solution.py:14
  77.3 0.0 copy-done
  77.3 4.7 %divide_convert_fusion = bf16[2,6400,128]{2,1,0:T(8,128)(2,1)S(1)} fusion(f32[2,6400,128]{2,1,0:T(8,128)} %param.4, bf16[2,6400,128]{2,1,0:T(8,128)(2,1)S(1)} %copy-done, f32[2,6400]{1,0:T(2,128)S(1)} %reduce_max.19), kind=kLoop, calls=%fused_computation | loop fusion | flops 6553600 | bytes 13158400 | tf_op jit(solution)/shard_map/convert_element_type | solution.py:30
  82.8 0.0 copy-start.1
  82.8 1.7 %copy-done.1 = bf16[32,2,200,128]{3,2,1,0:T(8,128)(2,1)} copy-done((bf16[32,2,200,128]{3,2,1,0:T(8,128)(2,1)}, bf16[32,2,200,128]{3,2,1,0:T(8,128)(2,1)S(1)}, u32[]{:S(2)}) %copy-start.1) | copy-done | bytes 3276824
  84.5 0.0 all-to-all-done.3
  84.5 5.0 %all-to-all-start.1 = ((bf16[32,2,200,128]{3,2,1,0:T(8,128)(2,1)}), bf16[32,2,200,128]{3,2,1,0:T(8,128)(2,1)S(1)}, u32[]{:S(2)}, u32[]{:S(2)}) async-start(bf16[32,2,200,128]{3,2,1,0:T(8,128)(2,1)} %copy-done.1), calls=%async_computation.1 | async-start | bytes 6553600 | tf_op jit(solution)/shard_map/all_to_all | solution.py:32
  89.5 0.7 reshape.23
  90.2 0.7 constant_dynamic-slice_fusion
  90.9 76.1 %all-to-all-done.1 = bf16[32,2,200,128]{3,2,1,0:T(8,128)(2,1)S(1)} async-done(((bf16[32,2,200,128]{3,2,1,0:T(8,128)(2,1)}), bf16[32,2,200,128]{3,2,1,0:T(8,128)(2,1)S(1)}, u32[]{:S(2)}, u32[]{:S(2)}) %all-to-all-start.1) | async-done | bytes 3276832 | tf_op jit(solution)/shard_map/all_to_all | solution.py:32
  167.0 2.1 %copy_bitcast_fusion = bf16[2,200,4096]{2,1,0:T(8,128)(2,1)} fusion(bf16[32,2,200,128]{3,2,1,0:T(8,128)(2,1)S(1)} %all-to-all-done.1), kind=kLoop, calls=%fused_computation.3 | loop fusion | bytes 6553600 | tf_op jit(solution)/shard_map/reshape | solution.py:31
  (32 shorter events, 0.6 us)
Async XLA Ops:
  1.9 18.8 %all-to-all-start.2 = ((bf16[32,128,2]{1,2,0:T(2,128)(2,1)}), bf16[32,128,2]{1,2,0:T(2,128)(2,1)S(1)}, u32[]{:S(2)}, u32[]{:S(2)}) async-start(bf16[32,128,2]{1,2,0:T(2,128)(2,1)} %broadcast_in_dim.12), calls=%async_computation.2 | async-start | bytes 32768 | tf_op jit(solution)/shard_map/all_to_all | solution.py:9
  18.7 58.6 %copy-start = (bf16[2,6400,128]{2,1,0:T(8,128)(2,1)S(1)}, bf16[2,6400,128]{2,1,0:T(8,128)(2,1)}, u32[]{:S(2)}) copy-start(bf16[2,6400,128]{2,1,0:T(8,128)(2,1)} %param.5) | copy-start | bytes 9830404
  68.6 15.9 %all-to-all-start.3 = ((bf16[8,4096,2]{1,2,0:T(2,128)(2,1)}), bf16[8,4096,2]{1,2,0:T(2,128)(2,1)S(1)}, u32[]{:S(2)}, u32[]{:S(2)}) async-start(bf16[8,4096,2]{1,2,0:T(2,128)(2,1)} %broadcast_in_dim.13), calls=%async_computation.3 | async-start | bytes 262144 | tf_op jit(solution)/shard_map/all_to_all | solution.py:9
  82.8 1.7 %copy-start.1 = (bf16[32,2,200,128]{3,2,1,0:T(8,128)(2,1)}, bf16[32,2,200,128]{3,2,1,0:T(8,128)(2,1)S(1)}, u32[]{:S(2)}) copy-start(bf16[32,2,200,128]{3,2,1,0:T(8,128)(2,1)S(1)} %fusion) | copy-start | bytes 9830404
  84.5 82.5 %all-to-all-start.1 = ((bf16[32,2,200,128]{3,2,1,0:T(8,128)(2,1)}), bf16[32,2,200,128]{3,2,1,0:T(8,128)(2,1)S(1)}, u32[]{:S(2)}, u32[]{:S(2)}) async-start(bf16[32,2,200,128]{3,2,1,0:T(8,128)(2,1)} %copy-done.1), calls=%async_computation.1 | async-start | bytes 6553600 | tf_op jit(solution)/shard_map/all_to_all | solution.py:32
